TPU v7x, 128 devices: a whole 4x4x4 slice. The times are simulated.
128 devices in a mesh: dp: 16 (over x_hi, z, core), tensor: 8 (over y, x_lo).
Axes of the slice: x: 4 (x_hi: 2, x_lo: 2; x = x_hi * 2 + x_lo), y: 4, z: 4, core: 2. Of those that a mesh axis runs over, the one named last changes fastest.
Arguments:
- latents: bfloat16 [176, 256, 640], P('dp', 'tensor'), may hold values from -6 to 6
- cotangent: bfloat16 [176, 256, 640], P('dp', 'tensor'), may hold values from -6 to 6
- trunc_steps: int32 [16], replicated, may hold values from 30 to 40, as said below
- timesteps: int32 [176], replicated, may hold values from 100 to 900
- tile_map: int32 [176], replicated, may hold values from 0 to 175, as said below
- gain: float32 [640], replicated, may hold values from 0.5 to 1.5
- w_value: bfloat16 [640, 2560], P(None, 'tensor'), may hold values from -0.25 to 0.25
- w_gate: bfloat16 [640, 2560], P(None, 'tensor'), may hold values from -0.25 to 0.25
- w_out: bfloat16 [640, 2560], P(None, 'tensor'), may hold values from -0.125 to 0.125
Outputs:
- placed_grad: bfloat16 [176, 256, 640], P('dp', 'tensor')
- grad_value: float32 [640, 2560], P('dp', 'tensor')
- grad_gate: float32 [640, 2560], P('dp', 'tensor')
- grad_out_proj: float32 [640, 2560], P('dp', 'tensor')
- grad_gain: float32 [640], replicated
Inputs may be any that keep to these rules, and one draw needn't show every extreme that they name: trunc_steps lies in 30 to 40, so a prompt has 1 to 11 live slots, its lowest ones. tile_map is a permutation of 0 to 175. Output slots g * 11 to g * 11 + 10 form group g; the live items go to the lowest slots of the groups, and each group receives the floor or the ceiling of (number of live items) / 16 of them.
All inputs are finite; a program needn't handle non-finite values.
Results may differ from a plain program's by a relative error of at most 0.0068.
Values may be sent and summed in bfloat16 or wider, within the bound.
A program may use at most 64 MiB of HBM per device.

v0:
```python
import functools
import jax
import jax.numpy as jnp
from jax import lax
from jax.sharding import Mesh
from jax.sharding import PartitionSpec as P

TENSOR = ("tensor_0", "tensor_1")
DP = ("dp_0", "dp_1", "dp_2")
DP_TENSOR = ("dp_0", "dp_1", "dp_2", "tensor_0", "tensor_1")
eps = 1e-05


def sent_together(arrays, axis, dim, along):
    widths = [a.shape[along] for a in arrays]
    both = jnp.concatenate(arrays, axis=along)
    whole = lax.all_gather(both, axis, axis=dim, tiled=True)
    return tuple(jnp.split(whole, [sum(widths[:k]) for k in range(1, len(widths))], axis=along))


def sum_by_axis(x, axes, dim):
    for axis in axes:
        x = lax.psum_scatter(x, axis, scatter_dimension=dim, tiled=True)
    return x


def in_one_piece(arrays, axis, dim, along):
    both = jnp.concatenate(arrays, axis=along)
    whole, at, gathered = (lax.psum_scatter(both, axis, scatter_dimension=dim, tiled=True), 0, [])
    for a in arrays:
        gathered.append(lax.slice_in_dim(whole, at, at + a.shape[along], axis=along))
        at += a.shape[along]
    return tuple(gathered)


def one_axis_at_a_time(x, axes):
    return functools.reduce(lax.psum, axes, x)


def alpha_bars():
    betas = jnp.linspace(0.00085**0.5, 0.012**0.5, 1000, dtype=jnp.float32) ** 2
    return jnp.exp(jnp.cumsum(jnp.log1p(-betas)))


def gelu_parts(inputs):
    cdf = 0.5 * (1.0 + lax.erf(inputs * 0.7071067811865476))
    density = jnp.exp(-0.5 * inputs * inputs) * 0.3989422804014327
    return (inputs * cdf, cdf + inputs * density)


def norm_backward(d_normed, grad_part, hat_part, inv_part, gain):
    d_hat = d_normed * gain
    input_grad = grad_part.astype(jnp.float32) + inv_part * (
        d_hat
        - jnp.mean(d_hat, axis=-1, keepdims=True)
        - hat_part * jnp.mean(d_hat * hat_part, axis=-1, keepdims=True)
    )
    gain_local = jnp.sum(d_normed * hat_part, axis=(0, 1))
    return (input_grad, gain_local)


def tile_backward(tiles, cot_tiles, slot_times, live_count, gain, w_value, w_gate, w_out):
    full_x, full_cot = sent_together((tiles, cot_tiles), TENSOR, 1, 0)
    width = full_x.shape[2]
    local_rows = tiles.shape[1]
    inner = w_value.shape[1]
    slot_total = full_x.shape[0]
    table = alpha_bars()
    picked = jnp.sum(
        jnp.where(
            slot_times[:, None] == jnp.arange(1000, dtype=jnp.int32)[None, :], table[None, :], 0.0
        ),
        axis=1,
    )
    noise_scale = jnp.sqrt(1.0 - picked)
    x_float = full_x.astype(jnp.float32)
    row_mean = jnp.mean(x_float, axis=-1, keepdims=True)
    centred = x_float - row_mean
    row_var = jnp.mean(centred * centred, axis=-1, keepdims=True)
    inv_std = lax.rsqrt(row_var + eps)
    x_hat = centred * inv_std
    normed = (x_hat * gain).astype(jnp.bfloat16)
    grad_tile = (full_cot.astype(jnp.float32) * noise_scale[:, None, None]).astype(jnp.bfloat16)
    first_dims = (((0,), (0,)), ((), ()))
    last_dims = (((1,), (1,)), ((), ()))

    def one_slot(slot_idx, carry):
        acc_wv, acc_wg, acc_wo, normed_buf = carry
        norm_tile = lax.dynamic_index_in_dim(normed, slot_idx, 0, keepdims=False)
        grad_one = lax.dynamic_index_in_dim(grad_tile, slot_idx, 0, keepdims=False)
        values_proj = jnp.dot(norm_tile, w_value, preferred_element_type=jnp.float32)
        gate_proj = jnp.dot(norm_tile, w_gate, preferred_element_type=jnp.float32)
        gelu_gate, gelu_slope = gelu_parts(gate_proj)
        hidden = (values_proj * gelu_gate).astype(jnp.bfloat16)
        d_hidden = jnp.dot(grad_one, w_out, preferred_element_type=jnp.float32)
        d_value = (d_hidden * gelu_gate).astype(jnp.bfloat16)
        d_gate = (d_hidden * values_proj * gelu_slope).astype(jnp.bfloat16)
        acc_wv = acc_wv + lax.dot_general(
            norm_tile, d_value, first_dims, preferred_element_type=jnp.float32
        )
        acc_wg = acc_wg + lax.dot_general(
            norm_tile, d_gate, first_dims, preferred_element_type=jnp.float32
        )
        acc_wo = acc_wo + lax.dot_general(
            grad_one, hidden, first_dims, preferred_element_type=jnp.float32
        )
        d_normed = lax.dot_general(d_value, w_value, last_dims, preferred_element_type=jnp.float32)
        d_normed = d_normed + lax.dot_general(
            d_gate, w_gate, last_dims, preferred_element_type=jnp.float32
        )
        normed_buf = lax.dynamic_update_index_in_dim(normed_buf, d_normed, slot_idx, 0)
        return (acc_wv, acc_wg, acc_wo, normed_buf)

    zero_w = jnp.zeros((width, inner), jnp.float32)
    init = (zero_w, zero_w, zero_w, jnp.zeros(full_x.shape, jnp.float32))
    acc_wv, acc_wg, acc_wo, normed_buf = lax.fori_loop(0, live_count, one_slot, init)
    offset = lax.axis_index(TENSOR) * local_rows
    hat_part = lax.dynamic_slice_in_dim(x_hat, offset, local_rows, 1)
    inv_part = lax.dynamic_slice_in_dim(inv_std, offset, local_rows, 1)
    grad_part = lax.dynamic_slice_in_dim(grad_tile, offset, local_rows, 1)
    slot_live = (jnp.arange(slot_total, dtype=jnp.int32) < live_count)[:, None, None]
    d_normed = sum_by_axis(normed_buf, TENSOR, 1)
    input_grad, gain_local = norm_backward(d_normed, grad_part, hat_part, inv_part, gain)
    input_grad = jnp.where(slot_live, input_grad, 0.0).astype(jnp.bfloat16)
    return (input_grad, (acc_wv, acc_wg, acc_wo), gain_local)


def per_device(latents, cotangent, trunc_steps, timesteps, tile_map, gain, w_value, w_gate, w_out):
    slot_total = latents.shape[0]
    total = tile_map.shape[0]
    my_group = lax.axis_index(DP)
    item_ids = jnp.arange(total, dtype=jnp.int32)
    live_all = (item_ids % slot_total < jnp.repeat(trunc_steps, slot_total) - 29).astype(jnp.int32)
    my_slots = my_group * slot_total + jnp.arange(slot_total, dtype=jnp.int32)
    is_mine = tile_map[:, None] == my_slots[None, :]
    dest_source = jnp.sum(jnp.where(is_mine, item_ids[:, None], 0), axis=0)
    slot_times = jnp.take(timesteps, my_slots)
    live_count = jnp.sum(jnp.take(live_all, my_slots))
    own_grad, weight_parts, gain_local = tile_backward(
        latents, cotangent, slot_times, live_count, gain, w_value, w_gate, w_out
    )
    every_grad = lax.all_gather(own_grad, DP, axis=0, tiled=True)
    placed_grad = jnp.take(every_grad, dest_source, axis=0)
    grad_value, grad_gate, grad_out_proj = in_one_piece(
        (weight_parts[0], weight_parts[1], weight_parts[2]), DP, 0, 1
    )
    grad_gain = one_axis_at_a_time(gain_local, DP_TENSOR)
    return (placed_grad, grad_value, grad_gate, grad_out_proj, grad_gain)


def solution(mesh):
    split = Mesh(
        mesh.devices.reshape(2, 4, 2, 4, 2), ("dp_0", "dp_1", "dp_2", "tensor_0", "tensor_1")
    )
    in_specs = (
        P(DP, TENSOR, None),
        P(DP, TENSOR, None),
        P(),
        P(),
        P(),
        P(),
        P(None, TENSOR),
        P(None, TENSOR),
        P(None, TENSOR),
    )
    out_specs = (P(DP, TENSOR, None), P(DP, TENSOR), P(DP, TENSOR), P(DP, TENSOR), P())
    return jax.shard_map(
        per_device, mesh=split, in_specs=in_specs, out_specs=out_specs, check_vma=False
    )
```

profile of v0, /device:TPU:1, one launch (start us, length us, event | category | flops | bytes accessed | tf_op | source)
XLA Modules:
  0.0 555.5 jit_solution(6888655949699349684)
XLA Ops:
  7.2 2.2 pad_maximum_fusion.1
  13.2 145.6 %all-gather.3.cloned.1.call-done = bf16[22,256,640]{2,1,0:T(8,128)(2,1)} async-done(((bf16[22,32,640]{2,1,0:T(8,128)(2,1)}), bf16[22,256,640]{2,1,0:T(8,128)(2,1)}) %all-gather.3.cloned.1.call-update) | async-done | bytes 7208976 | tf_op jit(solution)/shard_map/all_gather | solution.py:17
  158.9 2.7 convert_reduce_fusion
  161.6 3.2 fusion.34
  164.9 6.2 %fusion.32 = (f32[11,256,640]{2,1,0:T(8,128)}, bf16[11,256,640]{2,1,0:T(8,128)(2,1)}, bf16[11,256,640]{2,1,0:T(8,128)(2,1)}) fusion(f32[11,256]{1,0:T(8,128)S(1)} %add_rsqrt_fusion, f32[11,256]{1,0:T(8,128)S(1)} %broadcast_multiply_fusion, bf16[22,256,640]{2,1,0:T(8,128)(2,1)S(1)} %copy-done.3, f32[640]{0:T(1024)S(1)} %copy-done.4, f32[11]{0:T(128)S(1)} %subtract_sqrt_fusion), kind=kLoop, calls=%fused_computation.43 | loop fusion | flops 14417920 | bytes 21652012 | tf_op jit(solution)/shard_map/mul | solution.py:81
  171.3 3.6 broadcast_in_dim.86
  174.9 94.7 %while.16 = (s32[]{:T(128)}, f32[640,320]{0,1:T(8,128)S(1)}, f32[640,320]{0,1:T(8,128)S(1)}, f32[640,320]{0,1:T(8,128)S(1)}, f32[11,256,640]{2,1,0:T(8,128)}, /*...) while((s32[]{:T(128)}, f32[640,320]{0,1:T(8,128)S(1)}, ...), condition=%wide.region_8.10_spmd, body=%wide.region_7.9_spmd.sunk | while | flops 842424320 | bytes 15319243 | solution.py:116
  178.2 1.4 multiply_convert_fusion.8
  181.3 1.4 convolution_add_fusion.8
  182.7 1.4 convolution_add_fusion.9
  184.0 1.3 fusion.85
  187.3 1.3 fusion.83
  188.6 1.4 multiply_convert_fusion.8
  191.7 1.4 convolution_add_fusion.8
  193.1 1.4 convolution_add_fusion.9
  194.5 1.3 fusion.85
  196.5 1.3 fusion.82
  197.8 1.3 fusion.83
  199.1 1.4 multiply_convert_fusion.8
  202.2 1.4 convolution_add_fusion.8
  203.6 1.4 convolution_add_fusion.9
  204.9 1.3 fusion.85
  208.2 1.3 fusion.83
  209.6 1.4 multiply_convert_fusion.8
  212.7 1.4 convolution_add_fusion.8
  214.0 1.4 convolution_add_fusion.9
  215.4 1.3 fusion.85
  217.4 1.3 fusion.82
  220.0 1.4 multiply_convert_fusion.8
  223.1 1.4 convolution_add_fusion.8
  224.5 1.4 convolution_add_fusion.9
  225.9 1.3 fusion.85
  227.8 1.3 fusion.82
  230.4 1.4 multiply_convert_fusion.8
  233.6 1.4 convolution_add_fusion.8
  234.9 1.4 convolution_add_fusion.9
  236.3 1.3 fusion.85
  240.9 1.4 multiply_convert_fusion.8
  244.0 1.4 convolution_add_fusion.8
  245.4 1.4 convolution_add_fusion.9
  246.8 1.3 fusion.85
  250.0 1.3 fusion.83
  251.3 1.4 multiply_convert_fusion.8
  254.4 1.4 convolution_add_fusion.8
  255.8 1.4 convolution_add_fusion.9
  261.8 1.4 multiply_convert_fusion.8
  264.9 1.4 convolution_add_fusion.8
  266.3 1.4 convolution_add_fusion.9
  267.6 1.3 fusion.85
  269.7 92.8 %reduce-scatter.4.cloned.1.call-done = f32[11,64,640]{2,1,0:T(8,128)} async-done(((f32[11,256,640]{2,1,0:T(8,128)}), f32[11,64,640]{2,1,0:T(8,128)}) %reduce-scatter.4.cloned.1.call-update) | async-done | bytes 1802256 | tf_op jit(solution)/shard_map/reduce_scatter | solution.py:23
  362.9 1.3 copy.24
  364.6 3.3 pad_maximum_fusion
  368.7 27.1 %reduce-scatter.6.cloned.1.call-done = f32[11,32,640]{2,1,0:T(8,128)} async-done(((f32[11,64,640]{2,1,0:T(8,128)}), f32[11,32,640]{2,1,0:T(8,128)}) %reduce-scatter.6.cloned.1.call-update) | async-done | bytes 901136 | tf_op jit(solution)/shard_map/reduce_scatter | solution.py:23
  395.7 1.8 multiply_reduce_fusion
  397.5 2.7 select_convert_fusion
  400.4 72.0 %reduce-scatter.8.cloned.1.call-done = f32[40,960]{1,0:T(8,128)} async-done(((f32[640,960]{1,0:T(8,128)}), f32[40,960]{1,0:T(8,128)}) %reduce-scatter.8.cloned.1.call-update) | async-done | bytes 153616 | tf_op jit(solution)/shard_map/reduce_scatter | solution.py:29
  472.4 1.6 fusion.41
  474.0 5.3 psum.35
  479.3 8.1 %psum.36 = f32[640]{0:T(1024)S(1)} all-reduce(f32[640]{0:T(1024)S(1)} %psum.35), channel_id=1, replica_groups=mesh['dp_0'=2,'dp_1'=4,'dp_2'=2,'tensor_0'=4,'tensor_1'=2] {'dp_1'}, use_global_device_ids=true, to_apply=%region_16.18 | all-reduce | flops 640 | bytes 5120 | tf_op jit(solution)/shard_map/psum | solution.py:37
  487.4 8.1 %psum.37 = f32[640]{0:T(1024)S(1)} all-reduce(f32[640]{0:T(1024)S(1)} %psum.36), channel_id=1, replica_groups=mesh['dp_0'=2,'dp_1'=4,'dp_2'=2,'tensor_0'=4,'tensor_1'=2] {'dp_2'}, use_global_device_ids=true, to_apply=%region_17.19 | all-reduce | flops 640 | bytes 5120 | tf_op jit(solution)/shard_map/psum | solution.py:37
  495.5 8.8 %psum.38 = f32[640]{0:T(1024)S(1)} all-reduce(f32[640]{0:T(1024)S(1)} %psum.37), channel_id=1, replica_groups=mesh['dp_0'=2,'dp_1'=4,'dp_2'=2,'tensor_0'=4,'tensor_1'=2] {'tensor_0'}, use_global_device_ids=true, to_apply=%region_18.20 | all-reduce | flops 640 | bytes 5120 | tf_op jit(solution)/shard_map/psum | solution.py:37
  504.4 4.4 psum.39
  508.7 35.7 %all-gather.5.cloned.1.call-done = bf16[176,32,640]{2,1,0:T(8,128)(2,1)} async-done(((bf16[11,32,640]{2,1,0:T(8,128)(2,1)}), bf16[176,32,640]{2,1,0:T(8,128)(2,1)}) %all-gather.5.cloned.1.call-update) | async-done | bytes 7208976 | tf_op jit(solution)/shard_map/all_gather | solution.py:142
  544.4 3.7 gather_fusion
  (89 shorter events, 37.1 us)
Async XLA Ops:
  7.2 3.7 copy-start
  7.2 157.7 %copy-start.4 = (f32[640]{0:T(1024)S(1)}, f32[640]{0:T(1024)}, u32[]{:S(2)}) copy-start(f32[640]{0:T(1024)} %param.18) | copy-start | bytes 7684
  7.2 151.7 %all-gather.3.cloned.1.call-start = ((), (), s32[]{:S(2)}) async-start(), calls=%async_computation.3 | async-start | bytes 8110080 | tf_op jit(solution)/shard_map/all_gather | solution.py:17
  9.4 353.1 %reduce-scatter.4.cloned.1.call-start = ((), (), s32[]{:S(2)}) async-start(), calls=%async_computation.4 | async-start | bytes 9011200 | tf_op jit(solution)/shard_map/reduce_scatter | solution.py:23
  158.9 6.0 %copy-start.3 = (bf16[22,256,640]{2,1,0:T(8,128)(2,1)S(1)}, bf16[22,256,640]{2,1,0:T(8,128)(2,1)}, u32[]{:S(2)}) copy-start(bf16[22,256,640]{2,1,0:T(8,128)(2,1)} %all-gather.3.cloned.1.call-done) | copy-start | bytes 21626884
  171.1 3.8 copy-start.1
  171.1 3.8 copy-start.2
  269.6 126.1 %reduce-scatter.6.cloned.1.call-start = ((), (), s32[]{:S(2)}) async-start(), calls=%async_computation.5 | async-start | bytes 2703360 | tf_op jit(solution)/shard_map/reduce_scatter | solution.py:23
  362.5 109.9 %reduce-scatter.8.cloned.1.call-start = ((), (), s32[]{:S(2)}) async-start(), calls=%async_computation.7 | async-start | bytes 2785280 | tf_op jit(solution)/shard_map/reduce_scatter | solution.py:29
  364.2 36.0 %copy-start.5 = (s32[176]{0:T(256)S(1)}, s32[176]{0:T(256)}, u32[]{:S(2)}) copy-start(s32[176]{0:T(256)} %param.17) | copy-start | bytes 2116
  367.9 176.5 %all-gather.5.cloned.1.call-start = ((), (), s32[]{:S(2)}) async-start(), calls=%async_computation.6 | async-start | bytes 7659520 | tf_op jit(solution)/shard_map/all_gather | solution.py:142
Sparse Core Ops, SparseCore 0:
  9.6 149.1 all-gather.2
  269.8 92.7 reduce-scatter.3
  364.9 30.7 reduce-scatter.5
  399.6 72.7 reduce-scatter.7
  475.3 69.0 all-gather.4
where the time goes:
time: 558 us; the launch traced here: 555 us
  waiting for transfers between devices  373 us (67%)
  matrix products  87.6 us (16%)
  blocking collectives  34.7 us (6%)
  other arithmetic  25.8 us (5%)
  between operations  14 us (3%)
  local copies, waits for them, and re-layouts  12.8 us (2%)
  loops' own time  7.12 us (1%)
    all_gather x1, waiting for transfers between devices, sent_together(): whole = lax.all_gather(both, axis, axis=dim, tiled=True)  146 us
    reduce_scatter x2, waiting for transfers between devices, sum_by_axis(): x = lax.psum_scatter(x, axis, scatter_dimension=dim, tiled=True)  120 us
    reduce_scatter x1, waiting for transfers between devices, in_one_piece(): lax.psum_scatter(both, axis, scatter_dimension=dim, tiled=True)  72 us
    all_gather x1, waiting for transfers between devices, per_device(): every_grad = lax.all_gather(own_grad, DP, axis=0, tiled=True)  35.7 us
    psum x5, blocking collectives, one_axis_at_a_time(): return functools.reduce(lax.psum, axes, x)  34.7 us
    dot_general x9, matrix products, one_slot(): d_hidden = jnp.dot(grad_one, w_out, preferred_element_type=jnp.float32)  12.9 us
    dot_general x9, matrix products, one_slot(): lax.dot_general(norm_tile, d_gate, first_dims, preferred_element_type=jnp...  12.4 us
    dot_general x9, matrix products, one_slot(): lax.dot_general(grad_one, hidden, first_dims, preferred_element_type=jnp....  12.2 us
  transfers between devices with their start and end apart: 5, of which 5 were waited for; matrix products, arithmetic and copies ran while one was open for 3% of the time, Pallas kernels for 0%

commit v1 on v0

--- a/solution.py
+++ b/solution.py
@@ -139,7 +139,10 @@
     own_grad, weight_parts, gain_local = tile_backward(
         latents, cotangent, slot_times, live_count, gain, w_value, w_gate, w_out
     )
-    every_grad = lax.all_gather(own_grad, DP, axis=0, tiled=True)
+    count = lax.axis_size(DP)
+    blocks = jnp.stack([own_grad for _ in range(count)])
+    blocks = lax.all_to_all(blocks, DP, split_axis=0, concat_axis=0)
+    every_grad = jnp.concatenate(blocks, axis=0)
     placed_grad = jnp.take(every_grad, dest_source, axis=0)
     grad_value, grad_gate, grad_out_proj = in_one_piece(
         (weight_parts[0], weight_parts[1], weight_parts[2]), DP, 0, 1

time: 558 us -> 581 us (1.041)
  waiting for transfers between devices: 373 us -> 385 us
  starting transfers between devices: 0.2 us -> 7.57 us
    reduce_scatter x1, waiting for transfers between devices: 72 us -> 114 us  [in_one_piece(): lax.psum_scatter(both, axis, scatter_dimension=dim, tiled=True)]
    all_gather x1 -> x0, waiting for transfers between devices: 35.7 us -> none  [per_device(): every_grad = lax.all_gather(own_grad, DP, axis=0, tiled=True)]
    all_to_all x0 -> x1, starting transfers between devices: none -> 7.41 us  [per_device(): blocks = lax.all_to_all(blocks, DP, split_axis=0, concat_axis=0)]
  transfers between devices with their start and end apart: 5 -> 5, of which waited for: 5 -> 4; matrix products, arithmetic and copies ran while one was open for 3% -> 2% of each run, Pallas kernels for 0% -> 0%
where the time goes in v1:
time: 581 us; the launch traced here: 576 us
  waiting for transfers between devices  385 us (66%)
  matrix products  87.6 us (15%)
  blocking collectives  33.5 us (6%)
  other arithmetic  25 us (4%)
  local copies, waits for them, and re-layouts  16.4 us (3%)
  between operations  14 us (2%)
  starting transfers between devices  7.57 us (1%)
  loops' own time  7.12 us (1%)
    all_gather x1, waiting for transfers between devices, sent_together(): whole = lax.all_gather(both, axis, axis=dim, tiled=True)  146 us
    reduce_scatter x2, waiting for transfers between devices, sum_by_axis(): x = lax.psum_scatter(x, axis, scatter_dimension=dim, tiled=True)  125 us
    reduce_scatter x1, waiting for transfers between devices, in_one_piece(): lax.psum_scatter(both, axis, scatter_dimension=dim, tiled=True)  114 us
    psum x5, blocking collectives, one_axis_at_a_time(): return functools.reduce(lax.psum, axes, x)  33.5 us
    dot_general x9, matrix products, one_slot(): d_hidden = jnp.dot(grad_one, w_out, preferred_element_type=jnp.float32)  12.9 us
    dot_general x9, matrix products, one_slot(): lax.dot_general(norm_tile, d_gate, first_dims, preferred_element_type=jnp...  12.4 us
    dot_general x9, matrix products, one_slot(): lax.dot_general(grad_one, hidden, first_dims, preferred_element_type=jnp....  12.2 us
    dot_general x9, matrix products, one_slot(): lax.dot_general(d_gate, w_gate, last_dims, preferred_element_type=jnp.flo...  11.9 us
  transfers between devices with their start and end apart: 5, of which 4 were waited for; matrix products, arithmetic and copies ran while one was open for 2% of the time, Pallas kernels for 0%

profile of v1, /device:TPU:1, one launch (start us, length us, event | category | flops | bytes accessed | tf_op | source)
XLA Modules:
  0.0 576.2 jit_solution(11130507717078187981)
XLA Ops:
  7.2 2.2 pad_maximum_fusion.1
  13.3 145.6 %all-gather.2.cloned.1.call-done = bf16[22,256,640]{2,1,0:T(8,128)(2,1)} async-done(((bf16[22,32,640]{2,1,0:T(8,128)(2,1)}), bf16[22,256,640]{2,1,0:T(8,128)(2,1)}) %all-gather.2.cloned.1.call-update) | async-done | bytes 7208976 | tf_op jit(solution)/shard_map/all_gather | solution.py:17
  158.9 2.7 convert_reduce_fusion
  161.6 3.2 fusion.34
  164.9 6.2 %fusion.32 = (f32[11,256,640]{2,1,0:T(8,128)}, bf16[11,256,640]{2,1,0:T(8,128)(2,1)}, bf16[11,256,640]{2,1,0:T(8,128)(2,1)}) fusion(f32[11,256]{1,0:T(8,128)S(1)} %add_rsqrt_fusion, f32[11,256]{1,0:T(8,128)S(1)} %broadcast_multiply_fusion, bf16[22,256,640]{2,1,0:T(8,128)(2,1)S(1)} %copy-done.3, f32[640]{0:T(1024)S(1)} %copy-done.4, f32[11]{0:T(128)S(1)} %subtract_sqrt_fusion), kind=kLoop, calls=%fused_computation.43 | loop fusion | flops 14417920 | bytes 21652012 | tf_op jit(solution)/shard_map/mul | solution.py:81
  171.3 3.6 broadcast_in_dim.86
  174.9 94.7 %while.16 = (s32[]{:T(128)}, f32[640,320]{0,1:T(8,128)S(1)}, f32[640,320]{0,1:T(8,128)S(1)}, f32[640,320]{0,1:T(8,128)S(1)}, f32[11,256,640]{2,1,0:T(8,128)}, /*...) while((s32[]{:T(128)}, f32[640,320]{0,1:T(8,128)S(1)}, ...), condition=%wide.region_8.10_spmd, body=%wide.region_7.9_spmd.sunk | while | flops 842424320 | bytes 15319243 | solution.py:116
  175.6 1.3 fusion.82
  176.9 1.3 fusion.83
  178.2 1.4 multiply_convert_fusion.8
  181.3 1.4 convolution_add_fusion.8
  182.7 1.4 convolution_add_fusion.9
  184.0 1.3 fusion.85
  187.3 1.3 fusion.83
  188.6 1.4 multiply_convert_fusion.8
  191.7 1.4 convolution_add_fusion.8
  193.1 1.4 convolution_add_fusion.9
  194.5 1.3 fusion.85
  196.5 1.3 fusion.82
  197.8 1.3 fusion.83
  199.1 1.4 multiply_convert_fusion.8
  202.2 1.4 convolution_add_fusion.8
  203.6 1.4 convolution_add_fusion.9
  205.0 1.3 fusion.85
  208.3 1.3 fusion.83
  209.6 1.4 multiply_convert_fusion.8
  212.7 1.4 convolution_add_fusion.8
  214.1 1.4 convolution_add_fusion.9
  215.4 1.3 fusion.85
  220.0 1.4 multiply_convert_fusion.8
  223.1 1.4 convolution_add_fusion.8
  224.5 1.4 convolution_add_fusion.9
  225.9 1.3 fusion.85
  230.5 1.4 multiply_convert_fusion.8
  233.6 1.4 convolution_add_fusion.8
  234.9 1.4 convolution_add_fusion.9
  236.3 1.3 fusion.85
  240.9 1.4 multiply_convert_fusion.8
  244.0 1.4 convolution_add_fusion.8
  245.4 1.4 convolution_add_fusion.9
  246.8 1.3 fusion.85
  250.0 1.3 fusion.83
  251.4 1.4 multiply_convert_fusion.8
  254.5 1.4 convolution_add_fusion.8
  255.8 1.4 convolution_add_fusion.9
  261.8 1.4 multiply_convert_fusion.8
  264.9 1.4 convolution_add_fusion.8
  266.3 1.4 convolution_add_fusion.9
  267.6 1.3 fusion.85
  269.7 92.8 %reduce-scatter.4.cloned.1.call-done = f32[11,64,640]{2,1,0:T(8,128)} async-done(((f32[11,256,640]{2,1,0:T(8,128)}), f32[11,64,640]{2,1,0:T(8,128)}) %reduce-scatter.4.cloned.1.call-update) | async-done | bytes 1802256 | tf_op jit(solution)/shard_map/reduce_scatter | solution.py:23
  363.3 32.5 %reduce-scatter.6.cloned.1.call-done = f32[11,32,640]{2,1,0:T(8,128)} async-done(((f32[11,64,640]{2,1,0:T(8,128)}), f32[11,32,640]{2,1,0:T(8,128)}) %reduce-scatter.6.cloned.1.call-update) | async-done | bytes 901136 | tf_op jit(solution)/shard_map/reduce_scatter | solution.py:23
  395.7 1.8 multiply_reduce_fusion
  397.5 1.9 select_convert_fusion
  399.4 3.5 stack.2
  403.0 7.4 %all-to-all-start = ((bf16[16,11,32,640]{3,2,1,0:T(8,128)(2,1)}), bf16[16,11,32,640]{3,2,1,0:T(8,128)(2,1)}, u32[]{:S(2)}, u32[]{:S(2)}) async-start(bf16[16,11,32,640]{3,2,1,0:T(8,128)(2,1)} %stack.2), calls=%async_computation.2 | async-start | bytes 14417920 | tf_op jit(solution)/shard_map/all_to_all | solution.py:144
  412.4 3.2 pad_maximum_fusion
  415.8 114.1 %reduce-scatter.8.cloned.1.call-done = f32[40,960]{1,0:T(8,128)} async-done(((f32[640,960]{1,0:T(8,128)}), f32[40,960]{1,0:T(8,128)}) %reduce-scatter.8.cloned.1.call-update) | async-done | bytes 153616 | tf_op jit(solution)/shard_map/reduce_scatter | solution.py:29
  529.9 1.6 fusion.41
  531.6 5.3 psum.35
  536.8 8.0 %psum.36 = f32[640]{0:T(1024)S(1)} all-reduce(f32[640]{0:T(1024)S(1)} %psum.35), channel_id=1, replica_groups=mesh['dp_0'=2,'dp_1'=4,'dp_2'=2,'tensor_0'=4,'tensor_1'=2] {'dp_1'}, use_global_device_ids=true, to_apply=%region_16.18 | all-reduce | flops 640 | bytes 5120 | tf_op jit(solution)/shard_map/psum | solution.py:37
  544.8 7.5 %psum.37 = f32[640]{0:T(1024)S(1)} all-reduce(f32[640]{0:T(1024)S(1)} %psum.36), channel_id=1, replica_groups=mesh['dp_0'=2,'dp_1'=4,'dp_2'=2,'tensor_0'=4,'tensor_1'=2] {'dp_2'}, use_global_device_ids=true, to_apply=%region_17.19 | all-reduce | flops 640 | bytes 5120 | tf_op jit(solution)/shard_map/psum | solution.py:37
  552.3 8.5 %psum.38 = f32[640]{0:T(1024)S(1)} all-reduce(f32[640]{0:T(1024)S(1)} %psum.37), channel_id=1, replica_groups=mesh['dp_0'=2,'dp_1'=4,'dp_2'=2,'tensor_0'=4,'tensor_1'=2] {'tensor_0'}, use_global_device_ids=true, to_apply=%region_18.20 | all-reduce | flops 640 | bytes 5120 | tf_op jit(solution)/shard_map/psum | solution.py:37
  560.7 4.4 psum.39
  565.1 3.7 gather_fusion
  (89 shorter events, 38.4 us)
Async XLA Ops:
  7.2 3.7 copy-start
  7.2 157.7 %copy-start.4 = (f32[640]{0:T(1024)S(1)}, f32[640]{0:T(1024)}, u32[]{:S(2)}) copy-start(f32[640]{0:T(1024)} %param.18) | copy-start | bytes 7684
  7.2 151.7 %all-gather.2.cloned.1.call-start = ((), (), s32[]{:S(2)}) async-start(), calls=%async_computation.4 | async-start | bytes 8110080 | tf_op jit(solution)/shard_map/all_gather | solution.py:17
  9.4 353.1 %reduce-scatter.4.cloned.1.call-start = ((), (), s32[]{:S(2)}) async-start(), calls=%async_computation.5 | async-start | bytes 9011200 | tf_op jit(solution)/shard_map/reduce_scatter | solution.py:23
  158.9 6.0 %copy-start.3 = (bf16[22,256,640]{2,1,0:T(8,128)(2,1)S(1)}, bf16[22,256,640]{2,1,0:T(8,128)(2,1)}, u32[]{:S(2)}) copy-start(bf16[22,256,640]{2,1,0:T(8,128)(2,1)} %all-gather.2.cloned.1.call-done) | copy-start | bytes 21626884
  171.1 3.8 copy-start.1
  171.1 3.8 copy-start.2
  269.7 126.1 %reduce-scatter.6.cloned.1.call-start = ((), (), s32[]{:S(2)}) async-start(), calls=%async_computation.6 | async-start | bytes 2703360 | tf_op jit(solution)/shard_map/reduce_scatter | solution.py:23
  403.0 162.1 %all-to-all-start = ((bf16[16,11,32,640]{3,2,1,0:T(8,128)(2,1)}), bf16[16,11,32,640]{3,2,1,0:T(8,128)(2,1)}, u32[]{:S(2)}, u32[]{:S(2)}) async-start(bf16[16,11,32,640]{3,2,1,0:T(8,128)(2,1)} %stack.2), calls=%async_computation.2 | async-start | bytes 14417920 | tf_op jit(solution)/shard_map/all_to_all | solution.py:144
  410.4 5.2 copy-start.5
  410.4 119.6 %reduce-scatter.8.cloned.1.call-start = ((), (), s32[]{:S(2)}) async-start(), calls=%async_computation.7 | async-start | bytes 2785280 | tf_op jit(solution)/shard_map/reduce_scatter | solution.py:29
Sparse Core Ops, SparseCore 0:
  9.7 149.1 all-gather.1
  269.8 92.6 reduce-scatter.3
  364.9 30.7 reduce-scatter.5
  415.7 114.1 reduce-scatter.7
